TPU v7x, 256 devices: a whole 4x4x8 slice. The times are simulated.
256 devices in a mesh: dp: 32 (over z_hi, y, core), tensor: 8 (over z_lo, x).
Axes of the slice: x: 4, y: 4, z: 8 (z_hi: 4, z_lo: 2; z = z_hi * 2 + z_lo), core: 2. Of those that a mesh axis runs over, the one named last changes fastest.
Arguments:
- tokens: bfloat16 [8192, 2560], P('dp'), may hold values from -6 to 6
- target: bfloat16 [8192, 2560], P('dp'), may hold values from -6 to 6
- norm_gain: float32 [2560], replicated, may hold values from 0.25 to 1.75
- gate_weight: bfloat16 [2560, 7168], P('dp', 'tensor'), may hold values from -0.125 to 0.125
- up_weight: bfloat16 [2560, 7168], P('dp', 'tensor'), may hold values from -0.125 to 0.125
- down_weight: bfloat16 [7168, 2560], P('tensor', 'dp'), may hold values from -0.0625 to 0.0625
- tangent: bfloat16 [2560, 7168], P('dp', 'tensor'), may hold values from -0.125 to 0.125
- lengths: int32 [4], replicated, may hold values from 512 to 2048
- loss_scale: float32 [1], replicated, may hold values from 16 to 64
Outputs:
- hvp: float32 [2560, 7168], P('dp', 'tensor')
- rayleigh: float32 [1], replicated
All inputs are finite; a program needn't handle non-finite values.
Results may differ from a plain program's by a relative error of at most 0.017.
Values may be sent and summed in bfloat16 or wider, within the bound.
No kernel may reach another device: no remote copies, remote signals or barrier semaphores. Data moves between devices by JAX's collectives and lax.ppermute only.
A program may use at most 128 MiB of HBM per device.

v0:
```python
import jax
import jax.numpy as jnp
from jax import lax
from jax.sharding import Mesh
from jax.sharding import PartitionSpec as P

DP = ("dp_0", "dp_1", "dp_2")
TENSOR = ("tensor_0", "tensor_1")
DP_TENSOR = ("dp_0", "dp_1", "dp_2", "tensor_0", "tensor_1")


def in_one_piece(arrays, axis, dim, along):
    both = jnp.concatenate(arrays, axis=along)
    filled, at, outs = (lax.all_gather(both, axis, axis=dim, tiled=True), 0, [])
    for a in arrays:
        outs.append(lax.slice_in_dim(filled, at, at + a.shape[along], axis=along))
        at += a.shape[along]
    return tuple(outs)


def one_axis_at_a_time(value, axes):
    for axis in axes:
        value = lax.psum(value, axis)
    return value


def token_weights(first_pos, row_total, micro_len, lengths, loss_scale):
    position = first_pos + jnp.arange(row_total, dtype=jnp.int32)
    micro_id = position // micro_len
    offset = position - micro_id * micro_len
    onehot = micro_id[:, None] == jnp.arange(lengths.shape[0], dtype=jnp.int32)[None, :]
    live_len = jnp.sum(jnp.where(onehot, lengths[None, :], 0), axis=1)
    return jnp.where(
        offset < live_len, loss_scale[0] / live_len.astype(jnp.float32), jnp.float32(0.0)
    )


def shards(
    tokens, target, norm_gain, gate_weight, up_weight, down_weight, tangent, lengths, loss_scale
):
    row_count = tokens.shape[0]
    stream = tokens.astype(jnp.float32)
    mean_sq = jnp.mean(stream * stream, axis=-1, keepdims=True)
    normed = (stream * lax.rsqrt(mean_sq + 1e-06) * norm_gain[None, :]).astype(jnp.bfloat16)
    pieces = in_one_piece((gate_weight, up_weight, tangent), DP, 0, 1)
    columns = normed
    gate_pre, up_pre, gate_tan = tuple(
        (jnp.dot(columns, piece, preferred_element_type=jnp.float32) for piece in pieces)
    )
    sigma = jax.nn.sigmoid(gate_pre)
    slope = sigma * (1.0 + gate_pre * (1.0 - sigma))
    bend = sigma * (1.0 - sigma) * (2.0 + gate_pre * (1.0 - 2.0 * sigma))
    hidden = (gate_pre * sigma * up_pre).astype(jnp.bfloat16)
    hidden_tan = (slope * gate_tan * up_pre).astype(jnp.bfloat16)
    down_full = lax.all_gather(down_weight, DP, axis=1, tiled=True)
    stacked = jnp.dot(
        jnp.concatenate([hidden, hidden_tan], axis=0), down_full, preferred_element_type=jnp.float32
    )
    branch = stacked[:row_count]
    branch_tan = stacked[row_count:]
    micro_len = row_count * lax.axis_size(DP) // lengths.shape[0]
    first_row = lax.axis_index(DP) * row_count
    branch, branch_tan = (
        lax.psum(branch.astype(jnp.bfloat16), TENSOR).astype(jnp.float32),
        lax.psum(branch_tan.astype(jnp.bfloat16), TENSOR).astype(jnp.float32),
    )
    weight = token_weights(first_row, row_count, micro_len, lengths, loss_scale)
    output = stream + branch
    grad_out = (weight[:, None] * (output - target.astype(jnp.float32))).astype(jnp.bfloat16)
    grad_tan = (weight[:, None] * branch_tan).astype(jnp.bfloat16)
    grads = lax.dot_general(
        jnp.concatenate([grad_out, grad_tan], axis=0),
        down_full,
        (((1,), (1,)), ((), ())),
        preferred_element_type=jnp.float32,
    )
    grad_hid = grads[:row_count]
    hess_hid = grads[row_count:]
    hess_pre = (hess_hid * up_pre * slope + grad_hid * up_pre * bend * gate_tan).astype(
        jnp.bfloat16
    )
    tangent_f = tangent.astype(jnp.float32)
    tangent_sq = jnp.sum(tangent_f * tangent_f)
    curvature, squares = (
        one_axis_at_a_time(jnp.sum(gate_tan * hess_pre.astype(jnp.float32)), DP_TENSOR),
        one_axis_at_a_time(tangent_sq, DP_TENSOR),
    )
    columns = normed
    product = lax.dot_general(
        columns, hess_pre, (((0,), (0,)), ((), ())), preferred_element_type=jnp.float32
    )
    hvp = lax.psum_scatter(
        lax.optimization_barrier(product.astype(jnp.bfloat16))
        .astype(jnp.float32)
        .astype(jnp.bfloat16),
        DP,
        scatter_dimension=0,
        tiled=True,
    ).astype(jnp.float32)
    rayleigh = (curvature / squares).reshape(1)
    return (hvp, rayleigh)


def solution(mesh):
    torus = Mesh(
        mesh.devices.reshape(4, 4, 2, 2, 4), ("dp_0", "dp_1", "dp_2", "tensor_0", "tensor_1")
    )
    return jax.shard_map(
        shards,
        mesh=torus,
        in_specs=(
            P(DP, None),
            P(DP, None),
            P(),
            P(DP, TENSOR),
            P(DP, TENSOR),
            P(TENSOR, DP),
            P(DP, TENSOR),
            P(),
            P(),
        ),
        out_specs=(P(DP, TENSOR), P()),
        check_vma=False,
    )
```

profile of v0, /device:TPU:2, one launch (start us, length us, event | category | flops | bytes accessed | tf_op | source)
XLA Modules:
  0.0 400.0 jit_solution(3529880794193507350)
XLA Ops:
  7.2 1.9 pad_maximum_fusion
  9.2 0.7 all-gather.5.cloned.1.call-update
  10.0 1.7 fusion.6
  11.7 97.1 %all-gather.3.cloned.1.call-done = bf16[2560,2688]{1,0:T(8,128)(2,1)} async-done(((bf16[80,2688]{1,0:T(8,128)(2,1)}), bf16[2560,2688]{1,0:T(8,128)(2,1)}) %all-gather.3.cloned.1.call-update) | async-done | bytes 13762576 | tf_op jit(solution)/shard_map/all_gather | solution.py:14
  108.7 3.9 fusion
  112.6 3.9 fusion.4
  116.5 0.9 copy-done.2
  117.4 5.0 %multiply_convert_fusion.2 = (bf16[256,896]{1,0:T(8,128)(2,1)S(1)}, bf16[256,896]{1,0:T(8,128)(2,1)S(1)}, f32[256,896]{1,0:T(8,128)}) fusion(f32[256,896]{1,0:T(8,128)S(1)} %fusion.4, f32[256,896]{1,0:T(8,128)S(1)} %fusion, bf16[2560,2688]{1,0:T(8,128)(2,1)} %all-gather.3.cloned.1.call-done, bf16[256,2560]{1,0:T(8,128)(2,1)S(1)} %copy-done, ...), kind=kOutput, calls=%fused_computation.39 | convolution fusion | flops 1180008448 | bytes 9579520 | tf_op jit(solution)/shard_map/dot_general | solution.py:48
  122.4 58.1 %all-gather.5.cloned.1.call-done = bf16[896,2560]{0,1:T(8,128)(2,1)} async-done(((bf16[896,80]{0,1:T(8,128)(2,1)}), bf16[896,2560]{0,1:T(8,128)(2,1)}) %all-gather.5.cloned.1.call-update) | async-done | bytes 4587536 | tf_op jit(solution)/shard_map/all_gather | solution.py:55
  180.5 5.8 %convolution_convert_fusion.1 = bf16[512,2560]{1,0:T(8,128)(2,1)S(1)} fusion(bf16[896,2560]{0,1:T(8,128)(2,1)} %all-gather.5.cloned.1.call-done, bf16[256,896]{1,0:T(8,128)(2,1)S(1)} %get-tuple-element.19, bf16[256,896]{1,0:T(8,128)(2,1)S(1)} %get-tuple-element.18), kind=kOutput, calls=%fused_computation.7 | convolution fusion | flops 2351955968 | bytes 8126464 | tf_op jit(solution)/shard_map/dot_general | solution.py:56
  186.3 1.7 fusion.34
  189.0 86.6 %all-reduce.8.cloned.1.call-done = (bf16[256,2560]{1,0:T(8,128)(2,1)}, bf16[256,2560]{1,0:T(8,128)(2,1)}) async-done(((bf16[256,2560]{1,0:T(8,128)(2,1)}, bf16[256,2560]{1,0:T(8,128)(2,1)}), (bf16[256,2560]{1,0:T(8,128)(2,1)}, bf16[256,2560]{1,0:T(8,128)(2,1)})) %all-reduce.8.cloned.1.call-update) | async-done | bytes 2621456 | tf_op jit(solution)/shard_map/psum | solution.py:65
  275.5 2.5 fusion.11
  278.1 5.3 %fusion.12 = f32[512,896]{1,0:T(8,128)S(1)} fusion(bf16[896,2560]{0,1:T(8,128)(2,1)} %all-gather.5.cloned.1.call-done, bf16[256,2560]{1,0:T(8,128)(2,1)S(1)} %get-tuple-element.21, bf16[256,2560]{1,0:T(8,128)(2,1)S(1)} %get-tuple-element.20), kind=kOutput, calls=%fused_computation.17 | convolution fusion | flops 2354053120 | bytes 9043968 | tf_op jit(solution)/shard_map/dot_general | solution.py:71
  283.4 1.3 multiply_reduce_fusion
  284.7 3.7 convolution_convert_fusion
  288.5 0.9 copy-done.5
  290.0 12.9 %all-reduce.2 = (f32[]{:T(128)}, f32[]{:T(128)}) all-reduce(f32[]{:T(128)} %get-tuple-element.14, f32[]{:T(128)} %multiply_reduce_fusion.1), channel_id=1, replica_groups=mesh['dp_0'=4,'dp_1'=4,'dp_2'=2,'tensor_0'=2,'tensor_1'=4] {'dp_0'}, use_global_device_ids=true, to_apply=%region_6.7 | all-reduce | flops 2 | bytes 16 | tf_op jit(solution)/shard_map/psum | solution.py:23
  302.9 11.1 %all-reduce.1 = (f32[]{:T(128)}, f32[]{:T(128)}) all-reduce(f32[]{:T(128)} %get-tuple-element.6, f32[]{:T(128)} %get-tuple-element.7), channel_id=1, replica_groups=mesh['dp_0'=4,'dp_1'=4,'dp_2'=2,'tensor_0'=2,'tensor_1'=4] {'dp_1'}, use_global_device_ids=true, to_apply=%region_7.8 | all-reduce | flops 2 | bytes 16 | tf_op jit(solution)/shard_map/psum | solution.py:23
  314.0 3.1 all-reduce.4
  317.1 5.5 %all-reduce.3 = (f32[]{:T(128)}, f32[]{:T(128)}) all-reduce(f32[]{:T(128)} %get-tuple-element.10, f32[]{:T(128)} %get-tuple-element.11), channel_id=1, replica_groups=mesh['dp_0'=4,'dp_1'=4,'dp_2'=2,'tensor_0'=2,'tensor_1'=4] {'tensor_0'}, use_global_device_ids=true, to_apply=%region_9.10 | all-reduce | flops 2 | bytes 16 | tf_op jit(solution)/shard_map/psum | solution.py:23
  322.6 9.6 %all-reduce = (f32[]{:T(128)}, f32[]{:T(128)}) all-reduce(f32[]{:T(128)} %get-tuple-element.8, f32[]{:T(128)} %get-tuple-element.9), channel_id=1, replica_groups=mesh['dp_0'=4,'dp_1'=4,'dp_2'=2,'tensor_0'=2,'tensor_1'=4] {'tensor_1'}, use_global_device_ids=true, to_apply=%region_10.11 | all-reduce | flops 2 | bytes 16 | tf_op jit(solution)/shard_map/psum | solution.py:23
  333.5 57.2 %reduce-scatter.2.cloned.1.call-done = bf16[80,896]{1,0:T(8,128)(2,1)} async-done(((bf16[2560,896]{1,0:T(8,128)(2,1)}), bf16[80,896]{1,0:T(8,128)(2,1)}) %reduce-scatter.2.cloned.1.call-update) | async-done | bytes 143376 | tf_op jit(solution)/shard_map/reduce_scatter | solution.py:92
  390.7 1.6 convert_element_type.65
  (28 shorter events, 1.0 us)
Async XLA Ops:
  7.2 101.6 %copy-start = (bf16[256,2560]{1,0:T(8,128)(2,1)S(1)}, bf16[256,2560]{1,0:T(8,128)(2,1)}, u32[]{:S(2)}) copy-start(bf16[256,2560]{1,0:T(8,128)(2,1)} %param.9) | copy-start | bytes 3932164
  7.2 101.6 %copy-start.7 = (f32[2560]{0:T(1024)S(1)}, f32[2560]{0:T(1024)}, u32[]{:S(2)}) copy-start(f32[2560]{0:T(1024)} %param.11) | copy-start | bytes 30724
  7.2 101.5 %all-gather.3.cloned.1.call-start = ((), (), s32[]{:S(2)}) async-start(), calls=%async_computation.1 | async-start | bytes 14192640 | tf_op jit(solution)/shard_map/all_gather | solution.py:14
  9.2 171.3 %all-gather.5.cloned.1.call-start = ((), (), s32[]{:S(2)}) async-start(), calls=%async_computation.2 | async-start | bytes 4730880 | tf_op jit(solution)/shard_map/all_gather | solution.py:55
  9.9 265.6 %all-reduce.8.cloned.1.call-start = ((), (), s32[]{:S(2)}) async-start(), calls=%async_computation.4 | async-start | bytes 5242880 | tf_op jit(solution)/shard_map/psum | solution.py:65
  116.5 0.9 copy-start.2
  188.0 0.8 copy-start.6
  188.0 87.5 %copy-start.1 = (bf16[256,2560]{1,0:T(8,128)(2,1)S(1)}, bf16[256,2560]{1,0:T(8,128)(2,1)}, u32[]{:S(2)}) copy-start(bf16[256,2560]{1,0:T(8,128)(2,1)} %param.10) | copy-start | bytes 3932164
  188.0 202.7 %reduce-scatter.2.cloned.1.call-start = ((), (), s32[]{:S(2)}) async-start(), calls=%async_computation.3 | async-start | bytes 4730880 | tf_op jit(solution)/shard_map/reduce_scatter | solution.py:92
  278.1 5.3 %copy-start.3 = (f32[256,896]{1,0:T(8,128)S(1)}, f32[256,896]{1,0:T(8,128)}, u32[]{:S(2)}) copy-start(f32[256,896]{1,0:T(8,128)} %copy-done.2) | copy-start | bytes 2752516
  278.1 5.3 %copy-start.4 = (f32[256,896]{1,0:T(8,128)S(1)}, f32[256,896]{1,0:T(8,128)}, u32[]{:S(2)}) copy-start(f32[256,896]{1,0:T(8,128)} %get-tuple-element.22) | copy-start | bytes 2752516
  283.4 1.3 copy-start.8
  288.4 0.9 copy-start.5
Sparse Core Ops, SparseCore 0:
  10.6 98.0 all-gather.2
  111.3 69.1 all-gather.4
  188.2 87.3 all-reduce.7
  288.6 102.0 reduce-scatter.1
where the time goes:
time: 401 us; the launch traced here: 400 us
  waiting for transfers between devices  300 us (75%)
  blocking collectives  42.1 us (10%)
  matrix products  27.5 us (7%)
  between operations  17.1 us (4%)
  other arithmetic  9.85 us (2%)
    all_gather x1, waiting for transfers between devices, in_one_piece(): filled, at, outs = (lax.all_gather(both, axis, axis=dim, tiled=True), 0, [])  97.1 us
    psum x1, waiting for transfers between devices, shards(): lax.psum(branch_tan.astype(jnp.bfloat16), TENSOR).astype(jnp.float32)  86.6 us
    all_gather x1, waiting for transfers between devices, shards(): down_full = lax.all_gather(down_weight, DP, axis=1, tiled=True)  58.1 us
    reduce_scatter x1, waiting for transfers between devices, shards(): lax.psum_scatter(lax.optimization_barrier(product.astype(jnp.bfloat16)).a...  57.2 us
    psum x5, blocking collectives, one_axis_at_a_time(): value = lax.psum(value, axis)  42.1 us
    dot_general x3, matrix products, shards(): jnp.dot(columns, piece, preferred_element_type=jnp.float32)  12.7 us
  transfers between devices with their start and end apart: 4, of which 4 were waited for; matrix products, arithmetic and copies ran while one was open for 4% of the time, Pallas kernels for 0%

commit v1 on v0

--- a/solution.py
+++ b/solution.py
@@ -52,7 +52,7 @@
     bend = sigma * (1.0 - sigma) * (2.0 + gate_pre * (1.0 - 2.0 * sigma))
     hidden = (gate_pre * sigma * up_pre).astype(jnp.bfloat16)
     hidden_tan = (slope * gate_tan * up_pre).astype(jnp.bfloat16)
-    down_full = lax.all_gather(down_weight, DP, axis=1, tiled=True)
+    down_full = jnp.concatenate(lax.all_gather(down_weight, DP), axis=1)
     stacked = jnp.dot(
         jnp.concatenate([hidden, hidden_tan], axis=0), down_full, preferred_element_type=jnp.float32
     )

time: 401 us -> 411 us (1.025)
  waiting for transfers between devices: 300 us -> 306 us
  local copies, waits for them, and re-layouts: 3.52 us -> 9.36 us
    psum x1, waiting for transfers between devices: 86.6 us -> 95.8 us  [shards(): lax.psum(branch_tan.astype(jnp.bfloat16), TENSOR).astype(jnp.float32)]
    all_gather x1, waiting for transfers between devices: 97.1 us -> 88.8 us  [in_one_piece(): filled, at, outs = (lax.all_gather(both, axis, axis=dim, tiled=True), 0, [])]
    all_gather x1, waiting for transfers between devices: 58.1 us -> 63.8 us  [shards(): down_full = jnp.concatenate(lax.all_gather(down_weight, DP), axis=1)]
  transfers between devices with their start and end apart: 4 -> 4, of which waited for: 4 -> 4; matrix products, arithmetic and copies ran while one was open for 4% -> 3% of each run, Pallas kernels for 0% -> 0%
where the time goes in v1:
time: 411 us
  waiting for transfers between devices  306 us (74%)
  blocking collectives  42.2 us (10%)
  matrix products  25.4 us (6%)
  between operations  17.2 us (4%)
  other arithmetic  9.77 us (2%)
  local copies, waits for them, and re-layouts  9.36 us (2%)
    psum x1, waiting for transfers between devices, shards(): lax.psum(branch_tan.astype(jnp.bfloat16), TENSOR).astype(jnp.float32)  95.8 us
    all_gather x1, waiting for transfers between devices, in_one_piece(): filled, at, outs = (lax.all_gather(both, axis, axis=dim, tiled=True), 0, [])  88.8 us
    all_gather x1, waiting for transfers between devices, shards(): down_full = jnp.concatenate(lax.all_gather(down_weight, DP), axis=1)  63.8 us
    reduce_scatter x1, waiting for transfers between devices, shards(): lax.psum_scatter(lax.optimization_barrier(product.astype(jnp.bfloat16)).a...  57.1 us
    psum x5, blocking collectives, one_axis_at_a_time(): value = lax.psum(value, axis)  42.2 us
    dot_general x3, matrix products, shards(): jnp.dot(columns, piece, preferred_element_type=jnp.float32)  13.2 us
  transfers between devices with their start and end apart: 4, of which 4 were waited for; matrix products, arithmetic and copies ran while one was open for 3% of the time, Pallas kernels for 0%

profile of v1, /device:TPU:2, one launch (start us, length us, event | category | flops | bytes accessed | tf_op | source)
XLA Modules:
  0.0 410.5 jit_solution(14921401980029420283)
XLA Ops:
  7.9 1.9 pad_maximum_fusion
  9.9 1.7 fusion.6
  11.5 63.8 %all-gather.6.cloned.1.call-done = bf16[28672,80]{0,1:T(8,128)(2,1)} async-done(((bf16[896,80]{0,1:T(8,128)(2,1)}), bf16[28672,80]{0,1:T(8,128)(2,1)}) %all-gather.6.cloned.1.call-update) | async-done | bytes 4587536 | tf_op jit(solution)/shard_map/all_gather | solution.py:55
  75.4 3.0 copy.13
  78.5 3.7 copy.12
  82.2 88.8 %all-gather.4.cloned.1.call-done = bf16[2560,2688]{1,0:T(8,128)(2,1)} async-done(((bf16[80,2688]{1,0:T(8,128)(2,1)}), bf16[2560,2688]{1,0:T(8,128)(2,1)}) %all-gather.4.cloned.1.call-update) | async-done | bytes 13762576 | tf_op jit(solution)/shard_map/all_gather | solution.py:14
  171.0 3.9 fusion
  174.9 4.0 fusion.4
  179.0 5.3 %multiply_convert_fusion.2 = (bf16[256,896]{1,0:T(8,128)(2,1)S(1)}, bf16[256,896]{1,0:T(8,128)(2,1)S(1)}, f32[256,896]{1,0:T(8,128)}) fusion(f32[256,896]{1,0:T(8,128)S(1)} %fusion.4, f32[256,896]{1,0:T(8,128)S(1)} %fusion, bf16[2560,2688]{1,0:T(8,128)(2,1)} %all-gather.4.cloned.1.call-done, bf16[256,2560]{1,0:T(8,128)(2,1)S(1)} %copy-done, ...), kind=kOutput, calls=%fused_computation.39 | convolution fusion | flops 1180008448 | bytes 9579520 | tf_op jit(solution)/shard_map/dot_general | solution.py:48
  184.3 3.2 convolution_convert_fusion.1
  187.5 1.7 fusion.34
  190.4 95.8 %all-reduce.8.cloned.1.call-done = (bf16[256,2560]{1,0:T(8,128)(2,1)}, bf16[256,2560]{1,0:T(8,128)(2,1)}) async-done(((bf16[256,2560]{1,0:T(8,128)(2,1)}, bf16[256,2560]{1,0:T(8,128)(2,1)}), (bf16[256,2560]{1,0:T(8,128)(2,1)}, bf16[256,2560]{1,0:T(8,128)(2,1)})) %all-reduce.8.cloned.1.call-update) | async-done | bytes 2621456 | tf_op jit(solution)/shard_map/psum | solution.py:65
  286.1 2.5 fusion.11
  288.7 5.3 %fusion.12 = f32[512,896]{1,0:T(8,128)S(1)} fusion(bf16[896,2560]{0,1:T(8,128)(2,1)} %bitcast.14, bf16[256,2560]{1,0:T(8,128)(2,1)S(1)} %get-tuple-element.21, bf16[256,2560]{1,0:T(8,128)(2,1)S(1)} %get-tuple-element.20), kind=kOutput, calls=%fused_computation.17 | convolution fusion | flops 2354053120 | bytes 9043968 | tf_op jit(solution)/shard_map/dot_general | solution.py:71
  294.0 1.3 multiply_reduce_fusion
  295.3 3.7 convolution_convert_fusion
  299.1 0.9 copy-done.5
  300.6 12.9 %all-reduce.2 = (f32[]{:T(128)}, f32[]{:T(128)}) all-reduce(f32[]{:T(128)} %get-tuple-element.14, f32[]{:T(128)} %multiply_reduce_fusion.1), channel_id=1, replica_groups=mesh['dp_0'=4,'dp_1'=4,'dp_2'=2,'tensor_0'=2,'tensor_1'=4] {'dp_0'}, use_global_device_ids=true, to_apply=%region_6.7 | all-reduce | flops 2 | bytes 16 | tf_op jit(solution)/shard_map/psum | solution.py:23
  313.5 11.1 %all-reduce.1 = (f32[]{:T(128)}, f32[]{:T(128)}) all-reduce(f32[]{:T(128)} %get-tuple-element.6, f32[]{:T(128)} %get-tuple-element.7), channel_id=1, replica_groups=mesh['dp_0'=4,'dp_1'=4,'dp_2'=2,'tensor_0'=2,'tensor_1'=4] {'dp_1'}, use_global_device_ids=true, to_apply=%region_7.8 | all-reduce | flops 2 | bytes 16 | tf_op jit(solution)/shard_map/psum | solution.py:23
  324.6 3.1 all-reduce.4
  327.6 5.5 %all-reduce.3 = (f32[]{:T(128)}, f32[]{:T(128)}) all-reduce(f32[]{:T(128)} %get-tuple-element.10, f32[]{:T(128)} %get-tuple-element.11), channel_id=1, replica_groups=mesh['dp_0'=4,'dp_1'=4,'dp_2'=2,'tensor_0'=2,'tensor_1'=4] {'tensor_0'}, use_global_device_ids=true, to_apply=%region_9.10 | all-reduce | flops 2 | bytes 16 | tf_op jit(solution)/shard_map/psum | solution.py:23
  333.2 9.6 %all-reduce = (f32[]{:T(128)}, f32[]{:T(128)}) all-reduce(f32[]{:T(128)} %get-tuple-element.8, f32[]{:T(128)} %get-tuple-element.9), channel_id=1, replica_groups=mesh['dp_0'=4,'dp_1'=4,'dp_2'=2,'tensor_0'=2,'tensor_1'=4] {'tensor_1'}, use_global_device_ids=true, to_apply=%region_10.11 | all-reduce | flops 2 | bytes 16 | tf_op jit(solution)/shard_map/psum | solution.py:23
  344.2 57.1 %reduce-scatter.2.cloned.1.call-done = bf16[80,896]{1,0:T(8,128)(2,1)} async-done(((bf16[2560,896]{1,0:T(8,128)(2,1)}), bf16[80,896]{1,0:T(8,128)(2,1)}) %reduce-scatter.2.cloned.1.call-update) | async-done | bytes 143376 | tf_op jit(solution)/shard_map/reduce_scatter | solution.py:92
  401.2 1.6 convert_element_type.65
  (35 shorter events, 1.9 us)
Async XLA Ops:
  7.2 68.2 %all-gather.6.cloned.1.call-start = ((), (), s32[]{:S(2)}) async-start(), calls=%async_computation.3 | async-start | bytes 4730880 | tf_op jit(solution)/shard_map/all_gather | solution.py:55
  7.9 163.1 %all-gather.4.cloned.1.call-start = ((), (), s32[]{:S(2)}) async-start(), calls=%async_computation.1 | async-start | bytes 14192640 | tf_op jit(solution)/shard_map/all_gather | solution.py:14
  9.8 276.3 %all-reduce.8.cloned.1.call-start = ((), (), s32[]{:S(2)}) async-start(), calls=%async_computation.4 | async-start | bytes 5242880 | tf_op jit(solution)/shard_map/psum | solution.py:65
  78.4 92.6 %copy-start = (bf16[256,2560]{1,0:T(8,128)(2,1)S(1)}, bf16[256,2560]{1,0:T(8,128)(2,1)}, u32[]{:S(2)}) copy-start(bf16[256,2560]{1,0:T(8,128)(2,1)} %param.9) | copy-start | bytes 3932164
  78.4 92.6 %copy-start.7 = (f32[2560]{0:T(1024)S(1)}, f32[2560]{0:T(1024)}, u32[]{:S(2)}) copy-start(f32[2560]{0:T(1024)} %param.11) | copy-start | bytes 30724
  174.9 9.3 %slice-start = ((s8[4587520]{0:T(1024)(128)(4,1)}), s8[4194304]{0:T(1024)(128)(4,1)S(1)}, s32[]{:S(2)}) async-start(s8[4587520]{0:T(1024)(128)(4,1)} %bitcast.15), calls=%async_computation.5 | async-start | bytes 8388608
  179.0 5.3 %copy-start.2 = (f32[256,896]{1,0:T(8,128)}, f32[256,896]{1,0:T(8,128)S(1)}, u32[]{:S(2)}) copy-start(f32[256,896]{1,0:T(8,128)S(1)} %fusion.4) | copy-start | bytes 2752516
  179.0 5.3 %slice-start.1 = ((s8[4587520]{0:T(1024)(128)(4,1)}), s8[393216]{0:T(1024)(128)(4,1)S(1)}, s32[]{:S(2)}) async-start(s8[4587520]{0:T(1024)(128)(4,1)} %bitcast.15), calls=%async_computation.6 | async-start | bytes 786432
  189.2 1.1 copy-start.6
  189.2 96.9 %copy-start.1 = (bf16[256,2560]{1,0:T(8,128)(2,1)S(1)}, bf16[256,2560]{1,0:T(8,128)(2,1)}, u32[]{:S(2)}) copy-start(bf16[256,2560]{1,0:T(8,128)(2,1)} %param.10) | copy-start | bytes 3932164
  189.2 212.1 %reduce-scatter.2.cloned.1.call-start = ((), (), s32[]{:S(2)}) async-start(), calls=%async_computation.2 | async-start | bytes 4730880 | tf_op jit(solution)/shard_map/reduce_scatter | solution.py:92
  288.6 5.3 %copy-start.3 = (f32[256,896]{1,0:T(8,128)S(1)}, f32[256,896]{1,0:T(8,128)}, u32[]{:S(2)}) copy-start(f32[256,896]{1,0:T(8,128)} %copy-done.2) | copy-start | bytes 2752516
  288.7 5.3 %copy-start.4 = (f32[256,896]{1,0:T(8,128)S(1)}, f32[256,896]{1,0:T(8,128)}, u32[]{:S(2)}) copy-start(f32[256,896]{1,0:T(8,128)} %get-tuple-element.22) | copy-start | bytes 2752516
  294.0 1.3 copy-start.8
  299.0 0.9 copy-start.5
Sparse Core Ops, SparseCore 0:
  10.6 64.7 all-gather.5
  78.0 92.9 all-gather.3
  189.3 96.7 all-reduce.7
  299.2 102.0 reduce-scatter.1
